TPU v7x, 32 devices: a whole 2x2x4 slice. The times are simulated.
32 devices in a mesh: dp: 1, tp: 32 (over x, y, z, core).
Axes of the slice: x: 2, y: 2, z: 4, core: 2. Of those that a mesh axis runs over, the one named last changes fastest.
Arguments:
- x: bfloat16 [2048, 2048], P('dp')
- dy: bfloat16 [2048, 2048], P('dp')
- gate: bfloat16 [2048, 16384], P('dp', 'tp')
- up: bfloat16 [2048, 16384], P('dp', 'tp')
- w_gate: bfloat16 [2048, 16384], P(None, 'tp')
- w_up: bfloat16 [2048, 16384], P(None, 'tp')
- w_down: bfloat16 [16384, 2048], P('tp')
Outputs:
- output 1: bfloat16 [2048, 2048], P('dp')
- output 2: bfloat16 [2048, 16384], P('dp', 'tp')
- output 3: bfloat16 [2048, 16384], P('dp', 'tp')
- output 4: bfloat16 [16384, 2048], P(('dp', 'tp'))
All inputs are finite; a program needn't handle non-finite values.
Results may differ from a plain program's by a relative error of at most 0.012.
Values are sent between devices in bfloat16 or wider.
A program may use at most 2 GiB of HBM per device.

v0:
```python
import jax
import jax.numpy as jnp
from jax import lax
from jax.sharding import PartitionSpec as P


def act(gate, up):
    return jax.nn.gelu(gate) * up


def solution(mesh):
    def step(x, dy, gate, up, w_gate, w_up, w_down):
        hidden, back = jax.vjp(act, gate.astype(jnp.float32), up.astype(jnp.float32))
        d_hidden = jnp.dot(dy, w_down.T, preferred_element_type=jnp.float32)
        d_gate, d_up = (g.astype(jnp.bfloat16) for g in back(d_hidden))
        term = jnp.dot(d_gate, w_gate.T, preferred_element_type=jnp.float32) + jnp.dot(d_up, w_up.T, preferred_element_type=jnp.float32)
        dx = lax.psum(term.astype(jnp.bfloat16), "tp")
        dw_gate = jnp.dot(x.T, d_gate, preferred_element_type=jnp.float32)
        dw_up = jnp.dot(x.T, d_up, preferred_element_type=jnp.float32)
        dw_down = jnp.dot(hidden.astype(jnp.bfloat16).T, dy, preferred_element_type=jnp.float32)
        return dx, *(g.astype(jnp.bfloat16) for g in (dw_gate, dw_up, dw_down))

    tokens, columns, rows = P("dp", None), P(None, "tp"), P("tp", None)
    return jax.shard_map(
        step,
        mesh=mesh,
        in_specs=(tokens, tokens, P("dp", "tp"), P("dp", "tp"), columns, columns, rows),
        out_specs=(tokens, P("dp", "tp"), P("dp", "tp"), P(("dp", "tp"), None)),
        check_vma=False,
    )
```

profile of v0, /device:TPU:0, one launch (start us, length us, event | category | flops | bytes accessed | tf_op | source)
XLA Modules:
  0.0 243.8 jit_solution(2781184477468827126)
XLA Ops:
  7.2 0.0 copy-start
  7.2 0.0 all-reduce.2.cloned.1.call-start
  7.2 14.6 %fusion.4 = (bf16[2048,512]{1,0:T(8,128)(2,1)S(1)}, f32[2048,512]{1,0:T(8,128)}) fusion(bf16[2048,512]{1,0:T(8,128)(2,1)} %param.9, bf16[2048,512]{1,0:T(8,128)(2,1)} %param.10, bf16[2048,2048]{1,0:T(8,128)(2,1)} %param.8, bf16[512,2048]{1,0:T(8,128)(2,1)} %param.13), kind=kOutput, calls=%fused_computation.12 | convolution fusion | flops 4319084544 | bytes 20971520 | tf_op jit(solution)/shard_map/dot_general | solution.py:14
  21.8 0.0 copy-start.2
  21.8 0.0 copy-done
  21.8 8.3 %fusion.21 = f32[2048,2048]{1,0:T(8,128)} fusion(bf16[2048,512]{1,0:T(8,128)(2,1)S(1)} %get-tuple-element.8, bf16[2048,512]{1,0:T(8,128)(2,1)S(1)} %copy-done), kind=kOutput, calls=%fused_computation.32 | convolution fusion | flops 4294967296 | bytes 20971520 | tf_op jit(solution)/shard_map/dot_general | solution.py:16
  30.1 0.0 copy-done.2
  30.1 16.9 %add_convert_fusion = bf16[2048,2048]{1,0:T(8,128)(2,1)} fusion(f32[2048,2048]{1,0:T(8,128)} %fusion.21, bf16[2048,512]{1,0:T(8,128)(2,1)} %param.12, f32[2048,512]{1,0:T(8,128)} %get-tuple-element.9, bf16[2048,512]{1,0:T(8,128)(2,1)} %param.9), kind=kOutput, calls=%fused_computation | convolution fusion | flops 4314890240 | bytes 33554432 | tf_op jit(solution)/shard_map/dot_general | solution.py:16
  47.0 0.0 all-reduce.2.cloned.1.call-update
  47.1 8.6 %fusion.10 = bf16[2048,512]{0,1:T(8,128)(2,1)S(1)} fusion(bf16[2048,512]{1,0:T(8,128)(2,1)} %copy-done.2, bf16[2048,2048]{1,0:T(8,128)(2,1)} %param.7), kind=kOutput, calls=%fused_computation.22 | convolution fusion | flops 4296015872 | bytes 12582912 | tf_op jit(solution)/shard_map/dot_general | solution.py:18
  55.7 2.5 %copy.11 = bf16[2048,512]{1,0:T(8,128)(2,1)} copy(bf16[2048,512]{0,1:T(8,128)(2,1)S(1)} %fusion.10) | data formatting | bytes 4194304
  58.2 10.6 %fusion.11 = bf16[2048,512]{0,1:T(8,128)(2,1)S(1)} fusion(bf16[2048,2048]{1,0:T(8,128)(2,1)} %param.7, f32[2048,512]{1,0:T(8,128)} %get-tuple-element.9, bf16[2048,512]{1,0:T(8,128)(2,1)} %param.9), kind=kOutput, calls=%fused_computation.23 | convolution fusion | flops 4307550208 | bytes 16777216 | tf_op jit(solution)/shard_map/dot_general | solution.py:19
  68.8 2.5 %copy.12 = bf16[2048,512]{1,0:T(8,128)(2,1)} copy(bf16[2048,512]{0,1:T(8,128)(2,1)S(1)} %fusion.11) | data formatting | bytes 4194304
  71.3 11.6 %convolution_convert_fusion = bf16[512,2048]{1,0:T(8,128)(2,1)} fusion(bf16[2048,2048]{1,0:T(8,128)(2,1)} %param.8, bf16[2048,512]{1,0:T(8,128)(2,1)} %param.10, bf16[2048,512]{1,0:T(8,128)(2,1)} %param.9), kind=kOutput, calls=%fused_computation.19 | convolution fusion | flops 4308598784 | bytes 14680064 | tf_op jit(solution)/shard_map/dot_general | solution.py:20
  82.9 145.5 %all-reduce.2.cloned.1.call-done = bf16[2048,2048]{1,0:T(8,128)(2,1)} async-done(((bf16[2048,2048]{1,0:T(8,128)(2,1)}), bf16[2048,2048]{1,0:T(8,128)(2,1)}) %all-reduce.2.cloned.1.call-update) | async-done | bytes 8388624 | tf_op jit(solution)/shard_map/psum | solution.py:17
  228.4 0.0 copy-start.1
  228.4 8.6 %copy.14 = bf16[2048,2048]{1,0:T(8,128)(2,1)} copy(bf16[2048,2048]{1,0:T(8,128)(2,1)} %all-reduce.2.cloned.1.call-done) | data formatting | bytes 16777216
  237.0 0.0 copy-done.1
Async XLA Ops:
  7.2 14.6 %copy-start = (bf16[2048,512]{1,0:T(8,128)(2,1)S(1)}, bf16[2048,512]{1,0:T(8,128)(2,1)}, u32[]{:S(2)}) copy-start(bf16[2048,512]{1,0:T(8,128)(2,1)} %param.11) | copy-start | bytes 6291460
  7.2 221.2 %all-reduce.2.cloned.1.call-start = ((), (), s32[]{:S(2)}) async-start(), calls=%async_computation | async-start | bytes 16777216 | tf_op jit(solution)/shard_map/psum | solution.py:17
  21.8 8.3 %copy-start.2 = (bf16[2048,512]{1,0:T(8,128)(2,1)}, bf16[2048,512]{1,0:T(8,128)(2,1)S(1)}, u32[]{:S(2)}) copy-start(bf16[2048,512]{1,0:T(8,128)(2,1)S(1)} %get-tuple-element.8) | copy-start | bytes 6291460
  228.4 8.6 %copy-start.1 = (bf16[2048,512]{1,0:T(8,128)(2,1)S(1)}, bf16[2048,512]{1,0:T(8,128)(2,1)}, u32[]{:S(2)}) copy-start(bf16[2048,512]{1,0:T(8,128)(2,1)} %param.11) | copy-start | bytes 6291460
Sparse Core Ops, SparseCore 0:
  47.2 181.1 all-reduce.1
where the time goes:
time: 244 us
  waiting for transfers between devices  146 us (60%)
  matrix products  70.6 us (29%)
  between operations  14.1 us (6%)
  local copies, waits for them, and re-layouts  13.6 us (6%)
    psum x1, waiting for transfers between devices, step(): dx = lax.psum(term.astype(jnp.bfloat16), 'tp')  146 us
    dot_general x1, matrix products, step(): jnp.dot(d_up, w_up.T, preferred_element_type=jnp.float32)  16.9 us
    dot_general x1, matrix products, step(): d_hidden = jnp.dot(dy, w_down.T, preferred_element_type=jnp.float32)  14.6 us
    unnamed x9, local copies, waits for them, and re-layouts  13.6 us
    dot_general x1, matrix products, step(): jnp.dot(hidden.astype(jnp.bfloat16).T, dy, preferred_element_type=jnp.flo...  11.6 us
    dot_general x1, matrix products, step(): dw_up = jnp.dot(x.T, d_up, preferred_element_type=jnp.float32)  10.6 us
    dot_general x1, matrix products, step(): dw_gate = jnp.dot(x.T, d_gate, preferred_element_type=jnp.float32)  8.59 us
    dot_general x1, matrix products, step(): jnp.dot(d_gate, w_gate.T, preferred_element_type=jnp.float32)  8.33 us
  transfers between devices with their start and end apart: 1, of which 1 were waited for; matrix products, arithmetic and copies ran while one was open for 15% of the time, Pallas kernels for 0%

commit v1 on v0

v1 whole, which is shorter than its diff:
```python
import functools

import jax
import jax.numpy as jnp
from jax import lax
from jax.experimental import pallas as pl
from jax.experimental.pallas import tpu as pltpu
from jax.sharding import PartitionSpec as P

MESH = pl.DeviceIdType.MESH
BF = jnp.bfloat16
F32 = jnp.float32

ROWS = 2048
D = 2048
F = 512
R = 256
K = ROWS // R
HALF = D // 2
QC = HALF // 2
NB = 8
CB = D // NB

OFFS = {1: 1, 2: 3, 3: 5, 4: 7, 5: 9, 6: 11, 7: 13, 8: 15, 9: 17, 10: 18}
STEPS = K + OFFS[10]


def act(gate, up):
    return jax.nn.gelu(gate) * up


def dot_nt(a, b):
    return lax.dot_general(a, b, (((1,), (1,)), ((), ())), preferred_element_type=F32)


def dot_tn(a, b):
    return lax.dot_general(a, b, (((0,), (0,)), ((), ())), preferred_element_type=F32)


def kernel(
    x_hbm, dy_hbm, gate_hbm, up_hbm, wg_hbm, wu_hbm, wd_hbm,
    dx, dwg, dwu, dwd,
    wd, wcat, gu, hid_t, dyr, xc, dyc, own, cs, cr,
    s1, r1, s2, r2, s3, r3, s4, r4,
    ssem, rsem, wsem, gsem, dsem, bsem,
):
    me = lax.axis_index("tp")
    c = lax.rem(me, 2)
    zl = lax.rem(me // 2, 2)
    zh = lax.rem(me // 4, 2)
    y = lax.rem(me // 8, 2)
    x = me // 16
    pc = me + 1 - 2 * c
    pz1 = me + 2 - 4 * zl
    pz2 = me + 4 - 8 * zh
    py = me + 8 - 16 * y
    px = me + 16 - 32 * x

    def row_copy(k, slot):
        return pltpu.make_async_copy(dy_hbm.at[pl.ds(k * R, R)], dyr.at[slot], dsem.at[slot])

    def gate_copies(k):
        rows = pl.ds(k * R, R)
        return (
            pltpu.make_async_copy(gate_hbm.at[rows], gu.at[rows, pl.ds(0, F)], gsem.at[0, k]),
            pltpu.make_async_copy(up_hbm.at[rows], gu.at[rows, pl.ds(F, F)], gsem.at[1, k]),
        )

    w_copies = (
        pltpu.make_async_copy(wd_hbm, wd, wsem.at[0]),
        pltpu.make_async_copy(wg_hbm, wcat.at[:, pl.ds(0, F)], wsem.at[1]),
        pltpu.make_async_copy(wu_hbm, wcat.at[:, pl.ds(F, F)], wsem.at[2]),
    )

    def block_copy(which, j, slot):
        columns = pl.ds(j * CB, CB)
        src, dst = ((x_hbm, xc), (dy_hbm, dyc))[which]
        return pltpu.make_async_copy(src.at[:, columns], dst.at[slot], bsem.at[which, slot])

    row_copy(0, 0).start()
    w_copies[0].start()
    for cp in gate_copies(0):
        cp.start()
    w_copies[1].start()
    w_copies[2].start()
    row_copy(1, 1).start()
    for k in range(1, K):
        for cp in gate_copies(k):
            cp.start()
    for which in range(2):
        block_copy(which, 0, 0).start()

    barrier = pltpu.get_barrier_semaphore()
    partners = (pc, pz1, pz2, py, px)
    for p in partners:
        pl.semaphore_signal(barrier, inc=1, device_id=(0, p), device_id_type=MESH)
    pl.semaphore_wait(barrier, len(partners))

    def remote(src, dst, stage, color, k, p):
        return pltpu.make_async_remote_copy(
            src_ref=src, dst_ref=dst,
            send_sem=ssem.at[stage, color, k], recv_sem=rsem.at[stage, color, k],
            device_id=(0, p), device_id_type=MESH,
        )

    def m16(v):
        return pl.multiple_of(v, 16)

    own_col = pl.multiple_of(c * HALF, HALF)
    other_col = pl.multiple_of((1 - c) * HALF, HALF)

    BITS = ((x, y, px, py), (y, x, py, px))

    def core_copy(k):
        rows = pl.ds(pl.multiple_of(k * R, R), R)
        return remote(cs.at[rows], cr.at[rows], 0, 0, k, pc)

    def level_copy(level, e, k):
        s, r, p = (
            (s1, r1, BITS[e][2]), (s2, r2, pz1), (s3, r3, BITS[e][3]), (s4, r4, pz2),
        )[level - 1]
        n = R >> level
        rows = pl.ds(m16(k * n), n)
        return remote(s.at[e, rows], r.at[e, rows], level, e, k, p)

    def kept(level, e):
        b1, b3 = BITS[e][:2]
        bits = (b1, zl, b3, zh)
        return sum((bits[i] * (R >> (i + 1)) for i in range(level)), 0)

    def gather_copy(level, e, k, mine):
        p = (BITS[e][2], pz1, BITS[e][3], pz2)[level - 1]
        n = R >> level
        off = kept(level, e)
        if not mine:
            b = (BITS[e][0], zl, BITS[e][1], zh)[level - 1]
            off = off + (1 - 2 * b) * n
        view = dx.at[pl.ds(m16(k * R + off), n), pl.ds(pl.multiple_of(own_col + e * QC, QC), QC)]
        return remote(view, view, 9 - level, e, k, p)

    def out_copy(k, mine):
        view = dx.at[pl.ds(pl.multiple_of(k * R, R), R), pl.ds(own_col if mine else other_col, HALF)]
        return remote(view, view, 9, 0, k, pc)

    def total(level, e, k, off, n):
        cols = pl.ds(e * QC, QC)
        rows = pl.ds(m16(k * R + off), n)
        acc = own[rows, cols] + cr[rows, cols].astype(F32)
        recv = (r1, r2, r3, r4)
        for i in range(level):
            m = R >> (i + 1)
            local = off - kept(i + 1, e)
            acc = acc + recv[i][e, pl.ds(m16(k * m + local), n), :].astype(F32)
        return acc

    def reduce_stage(level, k):
        if level == 1:
            core_copy(k).wait_recv()
        for e in range(2):
            if level > 1:
                level_copy(level - 1, e, k).wait_recv()
            n = R >> level
            b = (BITS[e][0], zl, BITS[e][1], zh)[level - 1]
            off = kept(level - 1, e) + (1 - b) * n
            stage = (s1, s2, s3, s4)[level - 1]
            stage[e, pl.ds(m16(k * n), n), :] = total(level - 1, e, k, off, n).astype(BF)
            level_copy(level, e, k).start()

    def finish_stage(k):
        n = R >> 4
        for e in range(2):
            level_copy(4, e, k).wait_recv()
            off = kept(4, e)
            cols = pl.ds(pl.multiple_of(own_col + e * QC, QC), QC)
            dx[pl.ds(m16(k * R + off), n), cols] = total(4, e, k, off, n).astype(BF)
            gather_copy(4, e, k, True).start()

    def gather_stage(level, k):
        for e in range(2):
            gather_copy(level + 1, e, k, False).wait_recv()
            gather_copy(level, e, k, True).start()

    def last_stage(k):
        for e in range(2):
            gather_copy(1, e, k, False).wait_recv()
        out_copy(k, True).start()

    STAGES = {
        1: lambda k: reduce_stage(1, k),
        2: lambda k: reduce_stage(2, k),
        3: lambda k: reduce_stage(3, k),
        4: lambda k: reduce_stage(4, k),
        5: finish_stage,
        6: lambda k: gather_stage(3, k),
        7: lambda k: gather_stage(2, k),
        8: lambda k: gather_stage(1, k),
        9: last_stage,
        10: lambda k: out_copy(k, False).wait_recv(),
    }

    def compute_terms(k):
        slot = lax.rem(k, 2)
        r0 = pl.multiple_of(k * R, R)
        rows = pl.ds(r0, R)
        row_copy(k, slot).wait()
        for cp in gate_copies(k):
            cp.wait()

        @pl.when(k == 0)
        def _():
            w_copies[0].wait()

        for h in range(2):
            hc = pl.ds(h * (F // 2), F // 2)
            d_hidden = dot_nt(dyr[slot], wd[hc, :])
            g = gu[rows, pl.ds(h * (F // 2), F // 2)].astype(F32)
            u = gu[rows, pl.ds(F + h * (F // 2), F // 2)].astype(F32)
            hidden, back = jax.vjp(act, g, u)
            d_gate, d_up = back(d_hidden)
            gu[rows, pl.ds(h * (F // 2), F // 2)] = d_gate.astype(BF)
            gu[rows, pl.ds(F + h * (F // 2), F // 2)] = d_up.astype(BF)
            hid_t[hc, rows] = hidden.astype(BF).T

        @pl.when(k + 2 < K)
        def _():
            row_copy(k + 2, slot).start()

        @pl.when(k == 0)
        def _():
            w_copies[1].wait()
            w_copies[2].wait()

        d_cat = gu[rows, :]
        for n in range(2):
            cs[rows, pl.ds(n * QC, QC)] = dot_nt(d_cat, wcat[pl.ds(pl.multiple_of(other_col + n * QC, QC), QC), :]).astype(BF)
        core_copy(k).start()
        for n in range(2):
            own[rows, pl.ds(n * QC, QC)] = dot_nt(d_cat, wcat[pl.ds(pl.multiple_of(own_col + n * QC, QC), QC), :])

    def compute_weights(j, part):
        slot = lax.rem(j, 2)
        if part == 0:
            @pl.when(j + 1 < NB)
            def _():
                for which in range(2):
                    block_copy(which, j + 1, 1 - slot).start()

            block_copy(0, j, slot).wait()
            rows = pl.ds(pl.multiple_of(j * CB, CB), CB)
            dw = dot_tn(xc[slot], gu[...])
            dwg[rows, :] = dw[:, :F].astype(BF)
            dwu[rows, :] = dw[:, F:].astype(BF)
        else:
            block_copy(1, j, slot).wait()
            cols = pl.ds(pl.multiple_of(j * CB, CB), CB)
            dwd[:, cols] = jnp.dot(hid_t[...], dyc[slot], preferred_element_type=F32).astype(BF)

    def step(t, carry):
        def at(stage):
            k = t - OFFS[stage]

            @pl.when((k >= 0) & (k < K))
            def _():
                STAGES[stage](k)

        @pl.when(t < K)
        def _():
            compute_terms(t)

        for stage in (10, 9, 8, 7, 6):
            at(stage)

        @pl.when((t >= K) & (t < K + NB))
        def _():
            compute_weights(t - K, 0)

        for stage in (5, 4, 3, 2, 1):
            at(stage)

        @pl.when((t >= K) & (t < K + NB))
        def _():
            compute_weights(t - K, 1)

        return carry

    lax.fori_loop(0, STEPS, step, 0)

    def drain(k, carry):
        core_copy(k).wait_send()
        for e in range(2):
            for level in range(1, 5):
                level_copy(level, e, k).wait_send()
                gather_copy(level, e, k, True).wait_send()
        out_copy(k, True).wait_send()
        return carry

    lax.fori_loop(0, K, drain, 0)


def solution(mesh):
    def step(x, dy, gate, up, w_gate, w_up, w_down):
        def out(*shape):
            return pltpu.VMEM(shape, BF)

        def buf(*shape, dtype=BF):
            return pltpu.VMEM(shape, dtype)

        scratch = [
            buf(F, D), buf(D, 2 * F), buf(ROWS, 2 * F), buf(F, ROWS),
            buf(2, R, D), buf(2, ROWS, CB), buf(2, ROWS, CB),
            buf(ROWS, HALF, dtype=F32), buf(ROWS, HALF), buf(ROWS, HALF),
        ]
        for level in range(1, 5):
            scratch += [buf(2, ROWS >> level, QC), buf(2, ROWS >> level, QC)]
        sem = pltpu.SemaphoreType.DMA
        scratch += [sem((10, 2, K)), sem((10, 2, K)), sem((3,)), sem((2, K)), sem((2,)), sem((2, 2))]
        return tuple(
            pl.pallas_call(
                kernel,
                name="backward",
                out_shape=[out(ROWS, D), out(D, F), out(D, F), out(F, D)],
                in_specs=[pl.BlockSpec(memory_space=pl.ANY)] * 7,
                out_specs=[pl.BlockSpec(memory_space=pltpu.VMEM)] * 4,
                scratch_shapes=scratch,
                compiler_params=pltpu.CompilerParams(
                    collective_id=0, has_side_effects=True, vmem_limit_bytes=49 << 20
                ),
            )(x, dy, gate, up, w_gate, w_up, w_down)
        )

    tokens, columns, rows = P("dp", None), P(None, "tp"), P("tp", None)
    return jax.shard_map(
        step,
        mesh=mesh,
        in_specs=(tokens, tokens, P("dp", "tp"), P("dp", "tp"), columns, columns, rows),
        out_specs=(tokens, P("dp", "tp"), P("dp", "tp"), P(("dp", "tp"), None)),
        check_vma=False,
    )
```

time: 244 us -> 94.8 us (0.39)
  waiting for transfers between devices: 146 us -> 0 us
  Pallas kernels: 0 us -> 86.7 us
  matrix products: 70.6 us -> 0 us
  between operations: 14.1 us -> 0.64 us
  local copies, waits for them, and re-layouts: 13.6 us -> 7.35 us
    psum x1 -> x0, waiting for transfers between devices: 146 us -> none  [step(): dx = lax.psum(term.astype(jnp.bfloat16), 'tp')]
    pallas_call x0 -> x1, Pallas kernels: none -> 86.7 us  [step(): pl.pallas_call(kernel, name='backward', out_shape=[out(ROWS, D), out(D, F...]
    dot_general x6 -> x0, matrix products: 70.6 us -> none  [the longest x1 16.9 us: step(): jnp.dot(d_up, w_up.T, preferred_element_type=jnp.float32)]
    unnamed x9 -> x4, local copies, waits for them, and re-layouts: 13.6 us -> 7.35 us
  transfers between devices with their start and end apart: 1 -> 0, of which waited for: 1 -> 0; matrix products, arithmetic and copies ran while one was open for 15% -> 0% of each run, Pallas kernels for 0% -> 0%
where the time goes in v1:
time: 94.8 us; the launch traced here: 94.6 us
  Pallas kernels  86.7 us (91%)
  local copies, waits for them, and re-layouts  7.35 us (8%)
    pallas_call x1, Pallas kernels, step(): pl.pallas_call(kernel, name='backward', out_shape=[out(ROWS, D), out(D, F...  86.7 us
    unnamed x4, local copies, waits for them, and re-layouts  7.35 us

profile of v1, /device:TPU:0, one launch (start us, length us, event | category | flops | bytes accessed | tf_op | source)
XLA Modules:
  0.0 94.6 jit_solution(11883851744887124332)
XLA Ops:
  0.6 86.7 %backward.1 = (bf16[2048,2048]{1,0:T(8,128)(2,1)S(1)}, bf16[2048,512]{1,0:T(8,128)(2,1)S(1)}, bf16[2048,512]{1,0:T(8,128)(2,1)S(1)}, bf16[512,2048]{1,0:T(8,128)(2,1)S(1)}) custom-call(bf16[2048,2048]{1,0:T(8,128)(2,1)} %x_hbm.1, bf16[2048,2048]{1,0:T(8,128)(2,1)} %dy_hbm.1, bf16[2048,512]{1,0:T(8,128)(2,1)} %gate_hbm.1, bf16[2048,512]{1,0:T(8,128)(2,1)} %up_hbm.1, ...), custom_call_target="tpu_custom_call" | custom-call | tf_op jit(solution)/shard_map/backward/pallas_call | solution.py:318
  87.3 3.4 %copy.15 = bf16[2048,2048]{1,0:T(8,128)(2,1)} copy(bf16[2048,2048]{1,0:T(8,128)(2,1)S(1)} %get-tuple-element.4) | data formatting | bytes 16777216
  90.7 1.3 %copy.16 = bf16[2048,512]{1,0:T(8,128)(2,1)} copy(bf16[2048,512]{1,0:T(8,128)(2,1)S(1)} %get-tuple-element.5) | data formatting | bytes 4194304
  92.0 1.3 %copy.17 = bf16[2048,512]{1,0:T(8,128)(2,1)} copy(bf16[2048,512]{1,0:T(8,128)(2,1)S(1)} %get-tuple-element.6) | data formatting | bytes 4194304
  93.3 1.3 %copy.18 = bf16[512,2048]{1,0:T(8,128)(2,1)} copy(bf16[512,2048]{1,0:T(8,128)(2,1)S(1)} %get-tuple-element.7) | data formatting | bytes 4194304

commit v2 on v1

v2 whole, which is shorter than its diff:
```python
import functools

import jax
import jax.numpy as jnp
from jax import lax
from jax.experimental import pallas as pl
from jax.experimental.pallas import tpu as pltpu
from jax.sharding import PartitionSpec as P

MESH = pl.DeviceIdType.MESH
BF = jnp.bfloat16
F32 = jnp.float32

ROWS = 2048
D = 2048
F = 512
RC = 256
KC = ROWS // RC
K = 16
R = ROWS // K
PER = K // KC
HALF = D // 2
QC = HALF // 2
NB = 8
CB = D // NB

DELTAS = (2, 3, 3, 2, 3, 3, 6, 3, 9, 3)
OFFS = {i + 1: sum(DELTAS[: i + 1]) for i in range(10)}
STEPS = K + max(OFFS[10], 3 * NB)
NSLICE = 3 * NB


def block_sizes():
    sizes = [(R, QC)]
    for _ in range(4):
        n, m = sizes[-1]
        sizes.append((n // 2, m) if n > 16 else (n, m // 2))
    return sizes


SZ = block_sizes()


def act(gate, up):
    return jax.nn.gelu(gate) * up


def dot_nt(a, b):
    return lax.dot_general(a, b, (((1,), (1,)), ((), ())), preferred_element_type=F32)


def dot_tn(a, b):
    return lax.dot_general(a, b, (((0,), (0,)), ((), ())), preferred_element_type=F32)


def kernel(
    x_hbm, dy_hbm, gate_hbm, up_hbm, wg_hbm, wu_hbm, wd_hbm,
    dx, dwg, dwu, dwd,
    wd, wcat, gu, hid_t, dyr, xc, dyc, own, cs, cr,
    s1, r1, s2, r2, s3, r3, s4, r4,
    ssem, rsem, wsem, gsem, dsem, bsem,
):
    me = lax.axis_index("tp")
    c = lax.rem(me, 2)
    zl = lax.rem(me // 2, 2)
    zh = lax.rem(me // 4, 2)
    y = lax.rem(me // 8, 2)
    x = me // 16
    pc = me + 1 - 2 * c
    pz1 = me + 2 - 4 * zl
    pz2 = me + 4 - 8 * zh
    py = me + 8 - 16 * y
    px = me + 16 - 32 * x

    def row_copy(k, slot):
        return pltpu.make_async_copy(dy_hbm.at[pl.ds(k * RC, RC)], dyr.at[slot], dsem.at[slot])

    def gate_copies(k):
        rows = pl.ds(k * RC, RC)
        return (
            pltpu.make_async_copy(gate_hbm.at[rows], gu.at[rows, pl.ds(0, F)], gsem.at[0, k]),
            pltpu.make_async_copy(up_hbm.at[rows], gu.at[rows, pl.ds(F, F)], gsem.at[1, k]),
        )

    w_copies = (
        pltpu.make_async_copy(wd_hbm, wd, wsem.at[0]),
        pltpu.make_async_copy(wg_hbm, wcat.at[:, pl.ds(0, F)], wsem.at[1]),
        pltpu.make_async_copy(wu_hbm, wcat.at[:, pl.ds(F, F)], wsem.at[2]),
    )

    def block_copy(which, j, slot):
        columns = pl.ds(j * CB, CB)
        src, dst = ((x_hbm, xc), (dy_hbm, dyc))[which]
        return pltpu.make_async_copy(src.at[:, columns], dst.at[slot], bsem.at[which, slot])

    row_copy(0, 0).start()
    w_copies[0].start()
    for cp in gate_copies(0):
        cp.start()
    w_copies[1].start()
    w_copies[2].start()

    barrier = pltpu.get_barrier_semaphore()
    partners = (pc, pz1, pz2, py, px)
    for p in partners:
        pl.semaphore_signal(barrier, inc=1, device_id=(0, p), device_id_type=MESH)

    def remote(src, dst, stage, color, k, p):
        return pltpu.make_async_remote_copy(
            src_ref=src, dst_ref=dst,
            send_sem=ssem.at[stage, color], recv_sem=rsem.at[stage, color, k],
            device_id=(0, p), device_id_type=MESH,
        )

    def m16(v):
        return pl.multiple_of(v, 16)

    own_col = pl.multiple_of(c * HALF, HALF)
    other_col = pl.multiple_of((1 - c) * HALF, HALF)

    BITS = ((x, y, px, py), (y, x, py, px))

    def core_copy(k):
        rows = pl.ds(pl.multiple_of(k * R, R), R)
        return remote(cs.at[rows], cr.at[rows], 0, 0, k, pc)

    def m128(v):
        return v if isinstance(v, int) else pl.multiple_of(v, 128)

    def level_copy(level, e, k):
        s, r, p = (
            (s1, r1, BITS[e][2]), (s2, r2, pz1), (s3, r3, BITS[e][3]), (s4, r4, pz2),
        )[level - 1]
        n = SZ[level][0]
        rows = pl.ds(m16(k * n), n)
        return remote(s.at[e, rows], r.at[e, rows], level, e, k, p)

    def offset(level, e, flip=False):
        b1, b3 = BITS[e][:2]
        bits = (b1, zl, b3, zh)
        row = col = 0
        for i in range(level):
            b = bits[i]
            if flip and i == level - 1:
                b = 1 - b
            if SZ[i + 1][0] < SZ[i][0]:
                row = row + b * SZ[i + 1][0]
            else:
                col = col + b * SZ[i + 1][1]
        return row, col

    def gather_copy(level, e, k, mine):
        p = (BITS[e][2], pz1, BITS[e][3], pz2)[level - 1]
        n, m = SZ[level]
        row, col = offset(level, e, not mine)
        view = dx.at[pl.ds(m16(k * R + row), n), pl.ds(pl.multiple_of(own_col + e * QC + col, 128), m)]
        return remote(view, view, 9 - level, e, k, p)

    def out_copy(k, mine):
        view = dx.at[pl.ds(pl.multiple_of(k * R, R), R), pl.ds(own_col if mine else other_col, HALF)]
        return remote(view, view, 9, 0, k, pc)

    def total(level, e, k, off, size):
        (row, col), (n, m) = off, size
        rows, cols = pl.ds(m16(k * R + row), n), pl.ds(m128(e * QC + col), m)
        acc = own[rows, cols] + cr[rows, cols].astype(F32)
        recv = (r1, r2, r3, r4)
        for i in range(level):
            krow, kcol = offset(i + 1, e)
            rows = pl.ds(m16(k * SZ[i + 1][0] + row - krow), n)
            acc = acc + recv[i][e, rows, pl.ds(m128(col - kcol), m)].astype(F32)
        return acc

    def reduce_stage(level, k):
        if level == 1:
            core_copy(k).wait_recv()
        for e in range(2):
            if level > 1:
                level_copy(level - 1, e, k).wait_recv()
            n = SZ[level][0]
            stage = (s1, s2, s3, s4)[level - 1]
            stage[e, pl.ds(m16(k * n), n), :] = total(level - 1, e, k, offset(level, e, True), SZ[level]).astype(BF)
            level_copy(level, e, k).start()

    def finish_stage(k):
        n, m = SZ[4]
        for e in range(2):
            level_copy(4, e, k).wait_recv()
            row, col = offset(4, e)
            cols = pl.ds(pl.multiple_of(own_col + e * QC + col, 128), m)
            dx[pl.ds(m16(k * R + row), n), cols] = total(4, e, k, (row, col), (n, m)).astype(BF)
            gather_copy(4, e, k, True).start()

    def gather_stage(level, k):
        for e in range(2):
            gather_copy(level + 1, e, k, False).wait_recv()
            gather_copy(level, e, k, True).start()

    def last_stage(k):
        for e in range(2):
            gather_copy(1, e, k, False).wait_recv()
        out_copy(k, True).start()

    STAGES = {
        1: lambda k: reduce_stage(1, k),
        2: lambda k: reduce_stage(2, k),
        3: lambda k: reduce_stage(3, k),
        4: lambda k: reduce_stage(4, k),
        5: finish_stage,
        6: lambda k: gather_stage(3, k),
        7: lambda k: gather_stage(2, k),
        8: lambda k: gather_stage(1, k),
        9: last_stage,
        10: lambda k: out_copy(k, False).wait_recv(),
    }

    def compute_gates(k):
        slot = lax.rem(k, 2)
        rows = pl.ds(pl.multiple_of(k * RC, RC), RC)
        row_copy(k, slot).wait()
        for cp in gate_copies(k):
            cp.wait()

        for h in range(2):
            hc = pl.ds(h * (F // 2), F // 2)
            d_hidden = dot_nt(dyr[slot], wd[hc, :])
            g = gu[rows, pl.ds(h * (F // 2), F // 2)].astype(F32)
            u = gu[rows, pl.ds(F + h * (F // 2), F // 2)].astype(F32)
            hidden, back = jax.vjp(act, g, u)
            d_gate, d_up = back(d_hidden)
            gu[rows, pl.ds(h * (F // 2), F // 2)] = d_gate.astype(BF)
            gu[rows, pl.ds(F + h * (F // 2), F // 2)] = d_up.astype(BF)
            hid_t[hc, rows] = hidden.astype(BF).T

        @pl.when(k + 2 < KC)
        def _():
            row_copy(k + 2, slot).start()
            for cp in gate_copies(k + 2):
                cp.start()

    def compute_terms(k, part):
        rows = pl.ds(pl.multiple_of(k * RC, RC), RC)
        d_cat = gu[rows, :]
        if part == 0:
            for n in range(2):
                at = pl.ds(pl.multiple_of(other_col + n * QC, QC), QC)
                cs[rows, pl.ds(n * QC, QC)] = dot_nt(d_cat, wcat[at, :]).astype(BF)
        else:
            n = part - 1
            at = pl.ds(pl.multiple_of(own_col + n * QC, QC), QC)
            own[rows, pl.ds(n * QC, QC)] = dot_nt(d_cat, wcat[at, :])

    def start_core(k):
        for i in range(PER):
            core_copy(k * PER + i).start()

    def compute_weights(j, part):
        slot = lax.rem(j, 2)
        if part == 0:
            @pl.when(j + 1 < NB)
            def _():
                for which in range(2):
                    block_copy(which, j + 1, 1 - slot).start()

            block_copy(0, j, slot).wait()
        if part < 2:
            rows = pl.ds(pl.multiple_of(j * CB, CB), CB)
            (dwg, dwu)[part][rows, :] = dot_tn(xc[slot], gu[:, pl.ds(part * F, F)]).astype(BF)
        else:
            block_copy(1, j, slot).wait()
            cols = pl.ds(pl.multiple_of(j * CB, CB), CB)
            dwd[:, cols] = jnp.dot(hid_t[...], dyc[slot], preferred_element_type=F32).astype(BF)

    def when(condition, f, *args):
        @pl.when(condition)
        def _():
            f(*args)

    def step(t, carry):
        k, part = t // PER, lax.rem(t, PER)
        first = t < K
        def send_terms(k):
            compute_terms(k, 0)
            start_core(k)

        slices = [compute_gates, send_terms] + [functools.partial(compute_terms, part=i) for i in (1, 2)]
        for i in range(PER):
            def run(k, i=i):
                for f in slices[i * 4 // PER : (i + 1) * 4 // PER]:
                    f(k)

            when(first & (part == i) & ((k > 0) if i < max(1, PER // 2) else True), run, k)

        @pl.when(t == K - 2 * PER)
        def _():
            for which in range(2):
                block_copy(which, 0, 0).start()

        v = t - K
        j, part = v // 3, lax.rem(v, 3)
        second = (v >= 0) & (v < NSLICE)
        for i in range(3):
            when(second & (part == i), compute_weights, j, i)

        for stage in range(10, 0, -1):
            q = t - OFFS[stage]
            when((q >= 0) & (q < K), STAGES[stage], q)

        return carry

    w_copies[0].wait()
    compute_gates(0)
    row_copy(1, 1).start()
    for cp in gate_copies(1):
        cp.start()
    w_copies[1].wait()
    w_copies[2].wait()
    compute_terms(0, 0)
    pl.semaphore_wait(barrier, len(partners))
    start_core(0)

    lax.fori_loop(0, STEPS, step, 0)

    def sent(ref, stage, color):
        pltpu.make_async_copy(ref, ref, ssem.at[stage, color]).wait()

    sent(cs, 0, 0)
    sent(cs, 9, 0)
    for e in range(2):
        for level, ref in enumerate((s1, s2, s3, s4), 1):
            sent(ref.at[e], level, e)
            sent(ref.at[e], 9 - level, e)


def write_out(*refs):
    sources, targets, sem = refs[:4], refs[4:8], refs[8]
    copies = [pltpu.make_async_copy(s, t, sem.at[i]) for i, (s, t) in enumerate(zip(sources, targets))]
    for cp in copies:
        cp.start()
    for cp in copies:
        cp.wait()


def solution(mesh):
    def step(x, dy, gate, up, w_gate, w_up, w_down):
        def out(*shape):
            return pltpu.VMEM(shape, BF)

        def buf(*shape, dtype=BF):
            return pltpu.VMEM(shape, dtype)

        scratch = [
            buf(F, D), buf(D, 2 * F), buf(ROWS, 2 * F), buf(F, ROWS),
            buf(2, RC, D), buf(2, ROWS, CB), buf(2, ROWS, CB),
            buf(ROWS, HALF, dtype=F32), buf(ROWS, HALF), buf(ROWS, HALF),
        ]
        for n, m in SZ[1:]:
            scratch += [buf(2, K * n, m), buf(2, K * n, m)]
        sem = pltpu.SemaphoreType.DMA
        scratch += [sem((10, 2)), sem((10, 2, K)), sem((3,)), sem((2, KC)), sem((2,)), sem((2, 2))]
        held = (
            pl.pallas_call(
                kernel,
                name="backward",
                out_shape=[out(ROWS, D), out(D, F), out(D, F), out(F, D)],
                in_specs=[pl.BlockSpec(memory_space=pl.ANY)] * 7,
                out_specs=[pl.BlockSpec(memory_space=pltpu.VMEM)] * 4,
                scratch_shapes=scratch,
                compiler_params=pltpu.CompilerParams(
                    collective_id=0, has_side_effects=True, vmem_limit_bytes=49 << 20
                ),
            )(x, dy, gate, up, w_gate, w_up, w_down)
        )
        return tuple(
            pl.pallas_call(
                write_out,
                name="write_out",
                out_shape=[jax.ShapeDtypeStruct(v.shape, BF) for v in held],
                in_specs=[pl.BlockSpec(memory_space=pltpu.VMEM)] * 4,
                out_specs=[pl.BlockSpec(memory_space=pl.ANY)] * 4,
                scratch_shapes=[sem((4,))],
                compiler_params=pltpu.CompilerParams(vmem_limit_bytes=1 << 20),
            )(*(pltpu.with_memory_space_constraint(v, pltpu.VMEM) for v in held))
        )

    tokens, columns, rows = P("dp", None), P(None, "tp"), P("tp", None)
    return jax.shard_map(
        step,
        mesh=mesh,
        in_specs=(tokens, tokens, P("dp", "tp"), P("dp", "tp"), columns, columns, rows),
        out_specs=(tokens, P("dp", "tp"), P("dp", "tp"), P(("dp", "tp"), None)),
        check_vma=False,
    )
```

time: 94.8 us -> 89.6 us (0.945)
  local copies, waits for them, and re-layouts: 7.35 us -> 0 us
  Pallas kernels: 86.7 us -> 88.8 us
    unnamed x4 -> x0, local copies, waits for them, and re-layouts: 7.35 us -> none
    pallas_call x0 -> x1, Pallas kernels: none -> 5.38 us  [step(): pl.pallas_call(write_out, name='write_out', out_shape=[jax.ShapeDtypeStru...]
    pallas_call x1, Pallas kernels: 86.7 us -> 83.4 us  [step(): pl.pallas_call(kernel, name='backward', out_shape=[out(ROWS, D), out(D, F...]
where the time goes in v2:
time: 89.6 us; the launch traced here: 89.4 us
  Pallas kernels  88.8 us (99%)
    pallas_call x1, Pallas kernels, step(): pl.pallas_call(kernel, name='backward', out_shape=[out(ROWS, D), out(D, F...  83.4 us
    pallas_call x1, Pallas kernels, step(): pl.pallas_call(write_out, name='write_out', out_shape=[jax.ShapeDtypeStru...  5.38 us

profile of v2, /device:TPU:0, one launch (start us, length us, event | category | flops | bytes accessed | tf_op | source)
XLA Modules:
  0.0 89.4 jit_solution(14094690492785725297)
XLA Ops:
  0.6 83.4 %backward.1 = (bf16[2048,2048]{1,0:T(8,128)(2,1)S(1)}, bf16[2048,512]{1,0:T(8,128)(2,1)S(1)}, bf16[2048,512]{1,0:T(8,128)(2,1)S(1)}, bf16[512,2048]{1,0:T(8,128)(2,1)S(1)}) custom-call(bf16[2048,2048]{1,0:T(8,128)(2,1)} %x_hbm.1, bf16[2048,2048]{1,0:T(8,128)(2,1)} %dy_hbm.1, bf16[2048,512]{1,0:T(8,128)(2,1)} %gate_hbm.1, bf16[2048,512]{1,0:T(8,128)(2,1)} %up_hbm.1, ...), custom_call_target="tpu_custom_call" | custom-call | tf_op jit(solution)/shard_map/backward/pallas_call | solution.py:362
  84.0 5.4 %write_out.1 = (bf16[2048,2048]{1,0:T(8,128)(2,1)}, bf16[2048,512]{1,0:T(8,128)(2,1)}, bf16[2048,512]{1,0:T(8,128)(2,1)}, bf16[512,2048]{1,0:T(8,128)(2,1)}) custom-call(bf16[2048,2048]{1,0:T(8,128)(2,1)S(1)} %get-tuple-element.8.refs_0_, bf16[2048,512]{1,0:T(8,128)(2,1)S(1)} %get-tuple-element.9.refs_1_, bf16[2048,512]{1,0:T(8,128)(2,1)S(1)} %get-tuple-element.10.refs_2_, ...), custom_call_target="tpu_custom_call" | custom-call | tf_op jit(solution)/shard_map/write_out/pallas_call | solution.py:375

commit v3 on v2

v3 whole, which is shorter than its diff:
```python
import functools

import jax
import jax.numpy as jnp
from jax import lax
from jax.experimental import pallas as pl
from jax.experimental.pallas import tpu as pltpu
from jax.sharding import PartitionSpec as P

MESH = pl.DeviceIdType.MESH
BF = jnp.bfloat16
F32 = jnp.float32

ROWS = 2048
D = 2048
F = 512
RC = 256
KC = ROWS // RC
K = 16
R = ROWS // K
PER = K // KC
HALF = D // 2
QC = HALF // 2
NB = 8
CB = D // NB

DELTAS = (1, 3, 3, 3, 3, 3, 3, 3, 4, 2)
OFFS = {i + 1: sum(DELTAS[: i + 1]) for i in range(10)}
ST = 4
MID = K + ST * NB // 2
STEPS = max(MID, K + OFFS[10])
SLOTS = tuple(min(K, 2 * d + (4 if i == 0 else 1)) for i, d in enumerate(DELTAS))
BASE = tuple(sum(SLOTS[:i]) for i in range(11))


def block_sizes():
    sizes = [(R, QC)]
    for _ in range(4):
        n, m = sizes[-1]
        sizes.append((n // 2, m) if n > 16 else (n, m // 2))
    return sizes


SZ = block_sizes()


C0 = 0.7978845608028654
C1 = 0.044715


def gelu_and_slope(g):
    square = g * g
    th = jnp.tanh(C0 * (g + C1 * (square * g)))
    cdf = 0.5 * (1.0 + th)
    slope = cdf + (g * (0.5 * (1.0 - th * th))) * (C0 * (1.0 + (3.0 * C1) * square))
    return g * cdf, slope


def dot_nt(a, b):
    return lax.dot_general(a, b, (((1,), (1,)), ((), ())), preferred_element_type=F32)


def dot_tn(a, b):
    return lax.dot_general(a, b, (((0,), (0,)), ((), ())), preferred_element_type=F32)


def kernel(
    x_hbm, dy_hbm, gate_hbm, up_hbm, wg_hbm, wu_hbm, wd_hbm,
    dx, dwg, dwu, dwd,
    wd, wcat, gu, gelu, slope, hid_t, dyr, xc, dyc, own, cs, cr,
    s1, r1, s2, r2, s3, r3, s4, r4,
    ssem, rsem, wsem, gsem, dsem, bsem,
):
    me = lax.axis_index("tp")
    c = lax.rem(me, 2)
    zl = lax.rem(me // 2, 2)
    zh = lax.rem(me // 4, 2)
    y = lax.rem(me // 8, 2)
    x = me // 16
    pc = me + 1 - 2 * c
    pz1 = me + 2 - 4 * zl
    pz2 = me + 4 - 8 * zh
    py = me + 8 - 16 * y
    px = me + 16 - 32 * x

    def row_copy(k, slot):
        return pltpu.make_async_copy(dy_hbm.at[pl.ds(k * RC, RC)], dyr.at[slot], dsem.at[slot])

    def gate_copies(k):
        rows = pl.ds(k * RC, RC)
        return (
            pltpu.make_async_copy(gate_hbm.at[rows], gu.at[rows, pl.ds(0, F)], gsem.at[0, k]),
            pltpu.make_async_copy(up_hbm.at[rows], gu.at[rows, pl.ds(F, F)], gsem.at[1, k]),
        )

    w_copies = (
        pltpu.make_async_copy(wd_hbm, wd, wsem.at[0]),
        pltpu.make_async_copy(wg_hbm, wcat.at[:, pl.ds(0, F)], wsem.at[1]),
        pltpu.make_async_copy(wu_hbm, wcat.at[:, pl.ds(F, F)], wsem.at[2]),
    )

    def block_copy(which, j, slot):
        columns = pl.ds(j * CB, CB)
        src, dst = ((x_hbm, xc), (dy_hbm, dyc))[which]
        return pltpu.make_async_copy(src.at[:, columns], dst.at[slot], bsem.at[which, slot])

    for cp in gate_copies(0):
        cp.start()
    row_copy(0, 0).start()
    w_copies[0].start()

    barrier = pltpu.get_barrier_semaphore()
    partners = (pc, pz1, pz2, py, px)
    for p in partners:
        pl.semaphore_signal(barrier, inc=1, device_id=(0, p), device_id_type=MESH)

    def remote(src, dst, stage, color, k, p):
        return pltpu.make_async_remote_copy(
            src_ref=src, dst_ref=dst,
            send_sem=ssem.at[stage, color], recv_sem=rsem.at[slot(stage, k)],
            device_id=(0, p), device_id_type=MESH,
        )

    def m16(v):
        return pl.multiple_of(v, 16)

    own_col = pl.multiple_of(c * HALF, HALF)
    other_col = pl.multiple_of((1 - c) * HALF, HALF)

    def route(e, k):
        a, b, pa, pb = ((x, y, px, py), (y, x, py, px))[e]
        return (a, zl, b, zh), (pa, pz1, pb, pz2)

    def slot(stage, k):
        return BASE[stage] + lax.rem(k, SLOTS[stage])

    def core_copy(k):
        rows = pl.ds(pl.multiple_of(k * R, R), R)
        return remote(cs.at[rows], cr.at[rows], 0, 0, k, pc)

    def m128(v):
        return v if isinstance(v, int) else pl.multiple_of(v, 128)

    def level_copy(level, e, k):
        s, r = ((s1, r1), (s2, r2), (s3, r3), (s4, r4))[level - 1]
        p = route(e, k)[1][level - 1]
        n = SZ[level][0]
        rows = pl.ds(m16(k * n), n)
        return remote(s.at[e, rows], r.at[e, rows], level, e, k, p)

    def received(stage, k):
        level = stage if stage < 5 else 9 - stage
        if level == 0:
            ref = cr.at[pl.ds(m16(k * R), R)]
        else:
            n = SZ[level][0]
            ref = (r1, r2, r3, r4)[level - 1].at[:, pl.ds(m16(k * n), n)]
        pltpu.make_async_copy(ref, ref, rsem.at[slot(stage, k)]).wait()

    def offset(level, e, k, flip=False):
        bits = route(e, k)[0]
        row = col = 0
        for i in range(level):
            b = bits[i]
            if flip and i == level - 1:
                b = 1 - b
            if SZ[i + 1][0] < SZ[i][0]:
                row = row + b * SZ[i + 1][0]
            else:
                col = col + b * SZ[i + 1][1]
        return row, col

    def gather_copy(level, e, k):
        p = route(e, k)[1][level - 1]
        n, m = SZ[level]
        row, col = offset(level, e, k)
        view = dx.at[pl.ds(m16(k * R + row), n), pl.ds(pl.multiple_of(own_col + e * QC + col, 128), m)]
        return remote(view, view, 9 - level, e, k, p)

    def out_copy(k):
        view = dx.at[pl.ds(pl.multiple_of(k * R, R), R), pl.ds(own_col, HALF)]
        return remote(view, view, 9, 0, k, pc)

    def total(level, e, k, off, size):
        (row, col), (n, m) = off, size
        rows, cols = pl.ds(m16(k * R + row), n), pl.ds(m128(e * QC + col), m)
        acc = own[rows, cols] + cr[rows, cols].astype(F32)
        recv = (r1, r2, r3, r4)
        for i in range(level):
            krow, kcol = offset(i + 1, e, k)
            rows = pl.ds(m16(k * SZ[i + 1][0] + row - krow), n)
            acc = acc + recv[i][e, rows, pl.ds(m128(col - kcol), m)].astype(F32)
        return acc

    def reduce_stage(level, k):
        received(level - 1, k)
        for e in range(2):
            n = SZ[level][0]
            stage = (s1, s2, s3, s4)[level - 1]
            stage[e, pl.ds(m16(k * n), n), :] = total(level - 1, e, k, offset(level, e, k, True), SZ[level]).astype(BF)
            level_copy(level, e, k).start()

    def finish_stage(k):
        n, m = SZ[4]
        received(4, k)
        for e in range(2):
            row, col = offset(4, e, k)
            cols = pl.ds(pl.multiple_of(own_col + e * QC + col, 128), m)
            dx[pl.ds(m16(k * R + row), n), cols] = total(4, e, k, (row, col), (n, m)).astype(BF)
            gather_copy(4, e, k).start()

    def gather_stage(level, k):
        received(8 - level, k)
        for e in range(2):
            gather_copy(level, e, k).start()

    def last_stage(k):
        received(8, k)
        out_copy(k).start()

    STAGES = {
        1: lambda k: reduce_stage(1, k),
        2: lambda k: reduce_stage(2, k),
        3: lambda k: reduce_stage(3, k),
        4: lambda k: reduce_stage(4, k),
        5: finish_stage,
        6: lambda k: gather_stage(3, k),
        7: lambda k: gather_stage(2, k),
        8: lambda k: gather_stage(1, k),
        9: last_stage,
        10: lambda k: received(9, k),
    }

    def prepare(k, then=None):
        rows = pl.ds(pl.multiple_of(k * RC, RC), RC)
        for cp in gate_copies(k):
            cp.wait()
        if then is not None:
            then()
        value, slope[...] = gelu_and_slope(gu[rows, pl.ds(0, F)].astype(F32))
        gelu[...] = value
        hid_t[:, rows] = (value * gu[rows, pl.ds(F, F)].astype(F32)).astype(BF).T

    def compute_gates(k):
        half = lax.rem(k, 2)
        rows = pl.ds(pl.multiple_of(k * RC, RC), RC)
        row_copy(k, half).wait()
        d_hidden = dot_nt(dyr[half], wd[...])
        u = gu[rows, pl.ds(F, F)].astype(F32)
        gu[rows, pl.ds(0, F)] = ((d_hidden * u) * slope[...]).astype(BF)
        gu[rows, pl.ds(F, F)] = (d_hidden * gelu[...]).astype(BF)

        @pl.when(k + 2 < KC)
        def _():
            row_copy(k + 2, half).start()
            for cp in gate_copies(k + 2):
                cp.start()

    def compute_terms(k, part):
        rows = pl.ds(pl.multiple_of(k * RC, RC), RC)
        d_cat = gu[rows, :]
        if part == 0:
            cs[rows, :] = dot_nt(d_cat, wcat[pl.ds(other_col, HALF), :]).astype(BF)
        else:
            own[rows, :] = dot_nt(d_cat, wcat[pl.ds(own_col, HALF), :])

    def start_core(k):
        for i in range(PER):
            core_copy(k * PER + i).start()

    def compute_weights(j, part):
        half = lax.rem(j, 3)
        if part == 0:
            @pl.when(j + 2 < NB)
            def _():
                for which in range(2):
                    block_copy(which, j + 2, lax.rem(j + 2, 3)).start()

            block_copy(0, j, half).wait()
            rows = pl.ds(pl.multiple_of(j * CB, CB), CB)
            dw = dot_tn(xc[half], gu[...]).astype(BF)
            dwg[rows, :] = dw[:, :F]
            dwu[rows, :] = dw[:, F:]
        else:
            block_copy(1, j, half).wait()
            cols = pl.ds(pl.multiple_of(j * CB, CB), CB)
            dwd[:, cols] = jnp.dot(hid_t[...], dyc[half], preferred_element_type=F32).astype(BF)

    def when(condition, f, *args):
        @pl.when(condition)
        def _():
            f(*args)

    def send_terms(k):
        compute_terms(k, 0)
        start_core(k)

    def last_terms(k):
        compute_terms(k, 2)

        @pl.when(k + 1 < KC)
        def _():
            prepare(k + 1)

    def step(t, carry):
        k, odd = t // PER, lax.rem(t, PER) == 1
        first = t < K

        def stages(which):
            for stage in which:
                q = t - OFFS[stage]
                when((q >= 0) & (q < K), STAGES[stage], q)

        def slices(i):
            b = (t - K) * BPS + i
            for part in range(3):
                when((b >= 0) & (b < NSLICE) & (lax.rem(b, 3) == part), compute_weights, b // 3, part)

        when(first & jnp.logical_not(odd) & (k > 0), compute_gates, k)
        when(first & odd, compute_terms, k, 1)

        @pl.when(t == K - 2 * PER)
        def _():
            for which in range(2):
                block_copy(which, 0, 0).start()

        slices(0)
        stages((10, 9, 8, 7, 6))
        when(first & jnp.logical_not(odd) & (k > 0), send_terms, k)
        when(first & odd, last_terms, k)
        slices(1)
        stages((5, 4, 3, 2, 1))
        return carry

    LATE, EARLY = (10, 9, 8, 7, 6), (5, 4, 3, 2, 1)

    def stages(t, which, lo, hi):
        for stage in which:
            q = t - OFFS[stage]
            if hi - 1 - OFFS[stage] < 0 or lo - OFFS[stage] >= K:
                continue
            condition = None
            if lo < OFFS[stage]:
                condition = q >= 0
            if hi - 1 - OFFS[stage] >= K:
                condition = q < K if condition is None else condition & (q < K)
            if condition is None:
                STAGES[stage](q)
            else:
                when(condition, STAGES[stage], q)

    def chunk(k, more, lo, hi):
        t = PER * k
        compute_gates(k)
        stages(t, LATE, lo, hi)
        compute_terms(k, 0)
        start_core(k)
        stages(t, EARLY, lo, hi)
        stages(t + 1, LATE, lo, hi)
        compute_terms(k, 1)
        if more:
            prepare(k + 1)
        stages(t + 1, EARLY, lo, hi)

    def more_weights():
        w_copies[1].start()
        w_copies[2].start()

    prepare(0, more_weights)
    w_copies[0].wait()
    compute_gates(0)
    row_copy(1, 1).start()
    for cp in gate_copies(1):
        cp.start()
    w_copies[1].wait()
    w_copies[2].wait()
    compute_terms(0, 0)
    pl.semaphore_wait(barrier, len(partners))
    start_core(0)
    compute_terms(0, 1)
    prepare(1)
    stages(1, EARLY, 1, 2)

    def term_step(k, carry):
        chunk(k, True, PER, K - PER)
        return carry

    lax.fori_loop(1, KC - 1, term_step, 0)
    for j in range(2):
        for which in range(2):
            block_copy(which, j, j).start()
    chunk(jnp.int32(KC - 1), False, K - PER, K)

    def weight_step(i, carry):
        for n in range(2 * ST):
            for v in range(4):
                if v * 2 * ST // 4 == n:
                    compute_weights(2 * i + v // 2, v % 2)
            stages(K + ST * i + n // 2, (LATE, EARLY)[n % 2], K, MID)
        return carry

    lax.fori_loop(0, NB // 2, weight_step, 0)

    def tail_step(t, carry):
        stages(t, LATE + EARLY, MID, STEPS)
        return carry

    lax.fori_loop(MID, STEPS, tail_step, 0)

    def sent(ref, stage, color):
        pltpu.make_async_copy(ref, ref, ssem.at[stage, color]).wait()

    sent(cs, 0, 0)
    sent(cs, 9, 0)
    for e in range(2):
        for level, ref in enumerate((s1, s2, s3, s4), 1):
            sent(ref.at[e], level, e)
            sent(ref.at[e], 9 - level, e)


def write_out(*refs):
    sources, targets, sem = refs[:4], refs[4:8], refs[8]
    copies = [pltpu.make_async_copy(s, t, sem.at[i]) for i, (s, t) in enumerate(zip(sources, targets))]
    for cp in copies:
        cp.start()
    for cp in copies:
        cp.wait()


def solution(mesh):
    def step(x, dy, gate, up, w_gate, w_up, w_down):
        def out(*shape):
            return pltpu.VMEM(shape, BF)

        def buf(*shape, dtype=BF):
            return pltpu.VMEM(shape, dtype)

        scratch = [
            buf(F, D), buf(D, 2 * F), buf(ROWS, 2 * F), buf(RC, F, dtype=F32), buf(RC, F, dtype=F32), buf(F, ROWS),
            buf(2, RC, D), buf(3, ROWS, CB), buf(3, ROWS, CB),
            buf(ROWS, HALF, dtype=F32), buf(ROWS, HALF), buf(ROWS, HALF),
        ]
        for n, m in SZ[1:]:
            scratch += [buf(2, K * n, m), buf(2, K * n, m)]
        sem = pltpu.SemaphoreType.DMA
        scratch += [sem((10, 2)), sem((BASE[10],)), sem((3,)), sem((2, KC)), sem((2,)), sem((2, 3))]
        held = (
            pl.pallas_call(
                kernel,
                name="backward",
                out_shape=[out(ROWS, D), out(D, F), out(D, F), out(F, D)],
                in_specs=[pl.BlockSpec(memory_space=pl.ANY)] * 7,
                out_specs=[pl.BlockSpec(memory_space=pltpu.VMEM)] * 4,
                scratch_shapes=scratch,
                compiler_params=pltpu.CompilerParams(
                    collective_id=0, has_side_effects=True, vmem_limit_bytes=49 << 20
                ),
            )(x, dy, gate, up, w_gate, w_up, w_down)
        )
        return tuple(
            pl.pallas_call(
                write_out,
                name="write_out",
                out_shape=[jax.ShapeDtypeStruct(v.shape, BF) for v in held],
                in_specs=[pl.BlockSpec(memory_space=pltpu.VMEM)] * 4,
                out_specs=[pl.BlockSpec(memory_space=pl.ANY)] * 4,
                scratch_shapes=[sem((4,))],
                compiler_params=pltpu.CompilerParams(vmem_limit_bytes=1 << 20),
            )(*(pltpu.with_memory_space_constraint(v, pltpu.VMEM) for v in held))
        )

    tokens, columns, rows = P("dp", None), P(None, "tp"), P("tp", None)
    return jax.shard_map(
        step,
        mesh=mesh,
        in_specs=(tokens, tokens, P("dp", "tp"), P("dp", "tp"), columns, columns, rows),
        out_specs=(tokens, P("dp", "tp"), P("dp", "tp"), P(("dp", "tp"), None)),
        check_vma=False,
    )
```

time: 89.6 us -> 84.5 us (0.943)
  Pallas kernels: 88.8 us -> 83.8 us
    pallas_call x1, Pallas kernels: 83.4 us -> 78.4 us  [step(): pl.pallas_call(kernel, name='backward', out_shape=[out(ROWS, D), out(D, F...]
where the time goes in v3:
time: 84.5 us; the launch traced here: 84.4 us
  Pallas kernels  83.8 us (99%)
    pallas_call x1, Pallas kernels, step(): pl.pallas_call(kernel, name='backward', out_shape=[out(ROWS, D), out(D, F...  78.4 us
    pallas_call x1, Pallas kernels, step(): pl.pallas_call(write_out, name='write_out', out_shape=[jax.ShapeDtypeStru...  5.38 us

profile of v3, /device:TPU:0, one launch (start us, length us, event | category | flops | bytes accessed | tf_op | source)
XLA Modules:
  0.0 84.4 jit_solution(6437513439396885496)
XLA Ops:
  0.6 78.4 %backward.1 = (bf16[2048,2048]{1,0:T(8,128)(2,1)S(1)}, bf16[2048,512]{1,0:T(8,128)(2,1)S(1)}, bf16[2048,512]{1,0:T(8,128)(2,1)S(1)}, bf16[512,2048]{1,0:T(8,128)(2,1)S(1)}) custom-call(bf16[2048,2048]{1,0:T(8,128)(2,1)} %x_hbm.1, bf16[2048,2048]{1,0:T(8,128)(2,1)} %dy_hbm.1, bf16[2048,512]{1,0:T(8,128)(2,1)} %gate_hbm.1, bf16[2048,512]{1,0:T(8,128)(2,1)} %up_hbm.1, ...), custom_call_target="tpu_custom_call" | custom-call | tf_op jit(solution)/shard_map/backward/pallas_call | solution.py:448
  79.0 5.4 %write_out.1 = (bf16[2048,2048]{1,0:T(8,128)(2,1)}, bf16[2048,512]{1,0:T(8,128)(2,1)}, bf16[2048,512]{1,0:T(8,128)(2,1)}, bf16[512,2048]{1,0:T(8,128)(2,1)}) custom-call(bf16[2048,2048]{1,0:T(8,128)(2,1)S(1)} %get-tuple-element.8.refs_0_, bf16[2048,512]{1,0:T(8,128)(2,1)S(1)} %get-tuple-element.9.refs_1_, bf16[2048,512]{1,0:T(8,128)(2,1)S(1)} %get-tuple-element.10.refs_2_, ...), custom_call_target="tpu_custom_call" | custom-call | tf_op jit(solution)/shard_map/write_out/pallas_call | solution.py:461

commit v4 on v3

--- a/solution.py
+++ b/solution.py
@@ -26,10 +26,12 @@
 
 DELTAS = (1, 3, 3, 3, 3, 3, 3, 3, 4, 2)
 OFFS = {i + 1: sum(DELTAS[: i + 1]) for i in range(10)}
+LATE_CHUNKS = 4
+EARLY_CHUNKS = 4
 ST = 4
 MID = K + ST * NB // 2
 STEPS = max(MID, K + OFFS[10])
-SLOTS = tuple(min(K, 2 * d + (4 if i == 0 else 1)) for i, d in enumerate(DELTAS))
+SLOTS = tuple(K if i in (2, 3, 6, 7) else min(K, 2 * d + (4 if i == 0 else 1)) for i, d in enumerate(DELTAS))
 BASE = tuple(sum(SLOTS[:i]) for i in range(11))
 
 
@@ -129,7 +131,9 @@
 
     def route(e, k):
         a, b, pa, pb = ((x, y, px, py), (y, x, py, px))[e]
-        return (a, zl, b, zh), (pa, pz1, pb, pz2)
+        late = (k >= K - LATE_CHUNKS).astype(jnp.int32)
+        swap, pswap = late * (b - zl), late * (pb - pz1)
+        return (a, zl + swap, b - swap, zh), (pa, pz1 + pswap, pb - pswap, pz2)
 
     def slot(stage, k):
         return BASE[stage] + lax.rem(k, SLOTS[stage])
@@ -170,12 +174,20 @@
                 col = col + b * SZ[i + 1][1]
         return row, col
 
-    def gather_copy(level, e, k):
-        p = route(e, k)[1][level - 1]
+    def gather_copies(level, e, k):
+        bits, p = route(e, k)
+        crossed = ((k < EARLY_CHUNKS) | (k >= K - LATE_CHUNKS)).astype(jnp.int32)
         n, m = SZ[level]
         row, col = offset(level, e, k)
-        view = dx.at[pl.ds(m16(k * R + row), n), pl.ds(pl.multiple_of(own_col + e * QC + col, 128), m)]
-        return remote(view, view, 9 - level, e, k, p)
+        p = p[level - 1] if level in (1, 4) else p[level - 1] + crossed * (p[4 - level] - p[level - 1])
+        cols = pl.ds(pl.multiple_of(own_col + e * QC + col, 128), m)
+        rows = [pl.ds(m16(k * R + row), n)]
+        if level == 2:
+            half = n // 2
+            first = row + crossed * (offset(1, e, k)[0] + bits[2] * half - row)
+            stride = half + crossed * (n - half)
+            rows = [pl.ds(m16(k * R + first), half), pl.ds(m16(k * R + first + stride), half)]
+        return [remote(dx.at[r, cols], dx.at[r, cols], 9 - level, e, k, p) for r in rows]
 
     def out_copy(k):
         view = dx.at[pl.ds(pl.multiple_of(k * R, R), R), pl.ds(own_col, HALF)]
@@ -207,12 +219,14 @@
             row, col = offset(4, e, k)
             cols = pl.ds(pl.multiple_of(own_col + e * QC + col, 128), m)
             dx[pl.ds(m16(k * R + row), n), cols] = total(4, e, k, (row, col), (n, m)).astype(BF)
-            gather_copy(4, e, k).start()
+            for cp in gather_copies(4, e, k):
+                cp.start()
 
     def gather_stage(level, k):
         received(8 - level, k)
         for e in range(2):
-            gather_copy(level, e, k).start()
+            for cp in gather_copies(level, e, k):
+                cp.start()
 
     def last_stage(k):
         received(8, k)
@@ -379,7 +393,7 @@
     start_core(0)
     compute_terms(0, 1)
     prepare(1)
-    stages(1, EARLY, 1, 2)
+    stages(jnp.int32(1), EARLY, 1, 2)
 
     def term_step(k, carry):
         chunk(k, True, PER, K - PER)

time: 84.5 us -> 79.8 us (0.944)
  Pallas kernels: 83.8 us -> 78.8 us
    pallas_call x1, Pallas kernels: 78.4 us -> 73.5 us  [step(): pl.pallas_call(kernel, name='backward', out_shape=[out(ROWS, D), out(D, F...]
where the time goes in v4:
time: 79.8 us; the launch traced here: 79.6 us
  Pallas kernels  78.8 us (99%)
  between operations  0.8 us (1%)
    pallas_call x1, Pallas kernels, step(): pl.pallas_call(kernel, name='backward', out_shape=[out(ROWS, D), out(D, F...  73.5 us
    pallas_call x1, Pallas kernels, step(): pl.pallas_call(write_out, name='write_out', out_shape=[jax.ShapeDtypeStru...  5.38 us

profile of v4, /device:TPU:0, one launch (start us, length us, event | category | flops | bytes accessed | tf_op | source)
XLA Modules:
  0.0 79.6 jit_solution(11514426247146696712)
XLA Ops:
  0.6 73.5 %backward.1 = (bf16[2048,2048]{1,0:T(8,128)(2,1)S(1)}, bf16[2048,512]{1,0:T(8,128)(2,1)S(1)}, bf16[2048,512]{1,0:T(8,128)(2,1)S(1)}, bf16[512,2048]{1,0:T(8,128)(2,1)S(1)}) custom-call(bf16[2048,2048]{1,0:T(8,128)(2,1)} %x_hbm.1, bf16[2048,2048]{1,0:T(8,128)(2,1)} %dy_hbm.1, bf16[2048,512]{1,0:T(8,128)(2,1)} %gate_hbm.1, bf16[2048,512]{1,0:T(8,128)(2,1)} %up_hbm.1, ...), custom_call_target="tpu_custom_call" | custom-call | tf_op jit(solution)/shard_map/backward/pallas_call | solution.py:462
  74.1 5.4 %write_out.1 = (bf16[2048,2048]{1,0:T(8,128)(2,1)}, bf16[2048,512]{1,0:T(8,128)(2,1)}, bf16[2048,512]{1,0:T(8,128)(2,1)}, bf16[512,2048]{1,0:T(8,128)(2,1)}) custom-call(bf16[2048,2048]{1,0:T(8,128)(2,1)S(1)} %get-tuple-element.8.refs_0_, bf16[2048,512]{1,0:T(8,128)(2,1)S(1)} %get-tuple-element.9.refs_1_, bf16[2048,512]{1,0:T(8,128)(2,1)S(1)} %get-tuple-element.10.refs_2_, ...), custom_call_target="tpu_custom_call" | custom-call | tf_op jit(solution)/shard_map/write_out/pallas_call | solution.py:475

commit v5 on v4

--- a/solution.py
+++ b/solution.py
@@ -24,7 +24,7 @@
 NB = 8
 CB = D // NB
 
-DELTAS = (1, 3, 3, 3, 3, 3, 3, 3, 4, 2)
+DELTAS = (1, 3, 3, 3, 3, 3, 3, 4, 4, 2)
 OFFS = {i + 1: sum(DELTAS[: i + 1]) for i in range(10)}
 LATE_CHUNKS = 4
 EARLY_CHUNKS = 4
@@ -91,8 +91,8 @@
     def gate_copies(k):
         rows = pl.ds(k * RC, RC)
         return (
-            pltpu.make_async_copy(gate_hbm.at[rows], gu.at[rows, pl.ds(0, F)], gsem.at[0, k]),
-            pltpu.make_async_copy(up_hbm.at[rows], gu.at[rows, pl.ds(F, F)], gsem.at[1, k]),
+            pltpu.make_async_copy(gate_hbm.at[rows], gu.at[rows, pl.ds(0, F)], gsem.at[0, k % 2 if isinstance(k, int) else lax.rem(k, 2)]),
+            pltpu.make_async_copy(up_hbm.at[rows], gu.at[rows, pl.ds(F, F)], gsem.at[1, k % 2 if isinstance(k, int) else lax.rem(k, 2)]),
         )
 
     w_copies = (
@@ -405,15 +405,16 @@
             block_copy(which, j, j).start()
     chunk(jnp.int32(KC - 1), False, K - PER, K)
 
-    def weight_step(i, carry):
-        for n in range(2 * ST):
-            for v in range(4):
-                if v * 2 * ST // 4 == n:
-                    compute_weights(2 * i + v // 2, v % 2)
-            stages(K + ST * i + n // 2, (LATE, EARLY)[n % 2], K, MID)
+    def weight_step(j, carry):
+        for n in range(ST):
+            if n == 0:
+                compute_weights(j, 0)
+            if n == ST // 2:
+                compute_weights(j, 1)
+            stages(K + (ST // 2) * j + n // 2, (LATE, EARLY)[n % 2], K, MID)
         return carry
 
-    lax.fori_loop(0, NB // 2, weight_step, 0)
+    lax.fori_loop(0, NB, weight_step, 0)
 
     def tail_step(t, carry):
         stages(t, LATE + EARLY, MID, STEPS)
@@ -434,7 +435,11 @@
 
 def write_out(*refs):
     sources, targets, sem = refs[:4], refs[4:8], refs[8]
-    copies = [pltpu.make_async_copy(s, t, sem.at[i]) for i, (s, t) in enumerate(zip(sources, targets))]
+    copies = []
+    for s, t in zip(sources, targets):
+        n = s.shape[0] // 4
+        for i in range(4):
+            copies.append(pltpu.make_async_copy(s.at[pl.ds(i * n, n)], t.at[pl.ds(i * n, n)], sem.at[len(copies)]))
     for cp in copies:
         cp.start()
     for cp in copies:
@@ -457,7 +462,7 @@
         for n, m in SZ[1:]:
             scratch += [buf(2, K * n, m), buf(2, K * n, m)]
         sem = pltpu.SemaphoreType.DMA
-        scratch += [sem((10, 2)), sem((BASE[10],)), sem((3,)), sem((2, KC)), sem((2,)), sem((2, 3))]
+        scratch += [sem((10, 2)), sem((BASE[10],)), sem((3,)), sem((2, 2)), sem((2,)), sem((2, 3))]
         held = (
             pl.pallas_call(
                 kernel,
@@ -478,7 +483,7 @@
                 out_shape=[jax.ShapeDtypeStruct(v.shape, BF) for v in held],
                 in_specs=[pl.BlockSpec(memory_space=pltpu.VMEM)] * 4,
                 out_specs=[pl.BlockSpec(memory_space=pl.ANY)] * 4,
-                scratch_shapes=[sem((4,))],
+                scratch_shapes=[sem((16,))],
                 compiler_params=pltpu.CompilerParams(vmem_limit_bytes=1 << 20),
             )(*(pltpu.with_memory_space_constraint(v, pltpu.VMEM) for v in held))
         )

time: 79.8 us -> 79.8 us (level)
  no operation moved by 1% of the time
where the time goes in v5:
time: 79.8 us; the launch traced here: 79.4 us
  Pallas kernels  78.8 us (99%)
    pallas_call x1, Pallas kernels, step(): pl.pallas_call(kernel, name='backward', out_shape=[out(ROWS, D), out(D, F...  73.5 us
    pallas_call x1, Pallas kernels, step(): pl.pallas_call(write_out, name='write_out', out_shape=[jax.ShapeDtypeStru...  5.31 us

profile of v5, /device:TPU:0, one launch (start us, length us, event | category | flops | bytes accessed | tf_op | source)
XLA Modules:
  0.0 79.4 jit_solution(13442767354981195487)
XLA Ops:
  0.6 73.5 %backward.1 = (bf16[2048,2048]{1,0:T(8,128)(2,1)S(1)}, bf16[2048,512]{1,0:T(8,128)(2,1)S(1)}, bf16[2048,512]{1,0:T(8,128)(2,1)S(1)}, bf16[512,2048]{1,0:T(8,128)(2,1)S(1)}) custom-call(bf16[2048,2048]{1,0:T(8,128)(2,1)} %x_hbm.1, bf16[2048,2048]{1,0:T(8,128)(2,1)} %dy_hbm.1, bf16[2048,512]{1,0:T(8,128)(2,1)} %gate_hbm.1, bf16[2048,512]{1,0:T(8,128)(2,1)} %up_hbm.1, ...), custom_call_target="tpu_custom_call" | custom-call | tf_op jit(solution)/shard_map/backward/pallas_call | solution.py:467
  74.1 5.3 %write_out.1 = (bf16[2048,2048]{1,0:T(8,128)(2,1)}, bf16[2048,512]{1,0:T(8,128)(2,1)}, bf16[2048,512]{1,0:T(8,128)(2,1)}, bf16[512,2048]{1,0:T(8,128)(2,1)}) custom-call(bf16[2048,2048]{1,0:T(8,128)(2,1)S(1)} %get-tuple-element.8.refs_0_, bf16[2048,512]{1,0:T(8,128)(2,1)S(1)} %get-tuple-element.9.refs_1_, bf16[2048,512]{1,0:T(8,128)(2,1)S(1)} %get-tuple-element.10.refs_2_, ...), custom_call_target="tpu_custom_call" | custom-call | tf_op jit(solution)/shard_map/write_out/pallas_call | solution.py:480
